TPU v7x, 32 devices: a whole 2x2x4 slice. The times are simulated.
32 devices in a mesh: dp: 8 (over y, x, core), mp: 4 (over z).
Axes of the slice: x: 2, y: 2, z: 4, core: 2. Of those that a mesh axis runs over, the one named last changes fastest.
Arguments:
- inputs: bfloat16 [1024, 6144], P('dp'), may hold values from -6 to 6
- pre_act: bfloat16 [1024, 12288], P('dp', 'mp'), may hold values from -6 to 6
- out_grad: bfloat16 [1024, 6144], P('dp'), may hold values from -6 to 6
- w_in: bfloat16 [6144, 12288], P(None, 'mp'), may hold values from -0.109375 to 0.109375
- w_out: bfloat16 [12288, 6144], P('mp'), may hold values from -0.0546875 to 0.0546875
- master_in: float32 [6144, 12288], P('dp', 'mp'), may hold values from -0.3 to 0.3
- master_out: float32 [12288, 6144], P('mp', 'dp'), may hold values from -0.3 to 0.3
- row_in: float32 [6144], P('dp'), may hold values from 12.8 to 686.08
- col_in: float32 [12288], P('mp'), may hold values from 25 to 128
- row_out: float32 [12288], P('mp'), may hold values from 25.6 to 1372.16
- col_out: float32 [6144], P('dp'), may hold values from 51 to 256
Outputs:
- input_grad: bfloat16 [1024, 6144], P('dp', 'mp')
- new_master_in: float32 [6144, 12288], P('dp', 'mp')
- new_master_out: float32 [12288, 6144], P('mp', 'dp')
All inputs are finite; a program needn't handle non-finite values.
Results may differ from a plain program's by a relative error of at most 0.012.
Values may be sent and summed in bfloat16 or wider, within the bound.
A program may use at most 256 MiB of HBM per device.

v0:
```python
import math

import jax
import jax.numpy as jnp
from jax import lax
from jax.sharding import PartitionSpec as P

D = 6144
FF = 12288


decay_rate = 0.8
step_size = 0.05
tiny_square = 1e-30


def gelu_parts(pre):
    cumulative = 0.5 * (1.0 + jax.scipy.special.erf(pre * (1.0 / math.sqrt(2.0))))
    density = jnp.exp(-0.5 * pre * pre) * (1.0 / math.sqrt(2.0 * math.pi))
    return (pre * cumulative, cumulative + pre * density)


def contract_rows(left, right):
    return lax.dot_general(
        left, right, (((0,), (0,)), ((), ())), preferred_element_type=jnp.float32
    )


def body(
    inputs, pre_act, out_grad, w_in, w_out, master_in, master_out, row_in, col_in, row_out, col_out
):
    active, slope = gelu_parts(pre_act.astype(jnp.float32))
    hidden = active.astype(jnp.bfloat16)
    hid_grad = lax.dot_general(
        out_grad, w_out, (((1,), (1,)), ((), ())), preferred_element_type=jnp.float32
    )
    pre_grad = (hid_grad * slope).astype(jnp.bfloat16)
    input_cols = lax.psum_scatter(
        lax.dot_general(
            w_in, pre_grad, (((1,), (1,)), ((), ())), preferred_element_type=jnp.float32
        ),
        "mp",
        scatter_dimension=0,
        tiled=True,
    )
    input_grad = input_cols.T.astype(jnp.bfloat16)
    grad_in = lax.psum_scatter(
        contract_rows(inputs, pre_grad).astype(jnp.bfloat16), "dp", scatter_dimension=0, tiled=True
    ).astype(jnp.float32)
    grad_out = (
        lax.psum_scatter(
            contract_rows(out_grad, hidden).astype(jnp.bfloat16),
            "dp",
            scatter_dimension=0,
            tiled=True,
        )
        .astype(jnp.float32)
        .T
    )
    square_in = grad_in * grad_in + tiny_square
    square_out = grad_out * grad_out + tiny_square
    width_in, width_out = lax.psum((jnp.sum(square_in, axis=1), jnp.sum(square_out, axis=0)), "mp")
    hidden_in, hidden_out = lax.psum(
        (jnp.sum(square_in, axis=0), jnp.sum(square_out, axis=1)), "dp"
    )
    rows_in = decay_rate * row_in + (1.0 - decay_rate) * width_in / FF
    cols_in = decay_rate * col_in + (1.0 - decay_rate) * hidden_in / D
    rows_out = decay_rate * row_out + (1.0 - decay_rate) * hidden_out / D
    cols_out = decay_rate * col_out + (1.0 - decay_rate) * width_out / FF
    mean_in = lax.psum(jnp.sum(rows_in), "dp") / D
    mean_out = lax.psum(jnp.sum(rows_out), "mp") / FF
    update_in = grad_in / jnp.sqrt(rows_in[:, None] * cols_in[None, :] / mean_in)
    update_out = grad_out / jnp.sqrt(rows_out[:, None] * cols_out[None, :] / mean_out)
    new_master_in = master_in - step_size * update_in
    new_master_out = master_out - step_size * update_out
    return (input_grad, new_master_in, new_master_out)


def solution(mesh):
    in_specs = (
        P("dp", None),
        P("dp", "mp"),
        P("dp", None),
        P(None, "mp"),
        P("mp", None),
        P("dp", "mp"),
        P("mp", "dp"),
        P("dp"),
        P("mp"),
        P("mp"),
        P("dp"),
    )
    out_specs = (P("dp", "mp"), P("dp", "mp"), P("mp", "dp"))
    return jax.shard_map(body, mesh=mesh, in_specs=in_specs, out_specs=out_specs, check_vma=False)
```

profile of v0, /device:TPU:0, one launch (start us, length us, event | category | flops | bytes accessed | tf_op | source)
XLA Modules:
  0.0 646.3 jit_solution(12341110185972858558)
XLA Ops:
  7.2 0.0 copy-start
  7.2 0.0 reduce-scatter.4.cloned.1.call-start
  7.2 1.4 copy-done
  8.6 18.5 %fusion.10 = bf16[128,3072]{1,0:T(8,128)(2,1)S(1)} fusion(bf16[128,6144]{1,0:T(8,128)(2,1)S(1)} %copy-done, bf16[3072,6144]{1,0:T(8,128)(2,1)} %param.15, bf16[128,3072]{1,0:T(8,128)(2,1)} %param.12), kind=kOutput, calls=%fused_computation.18 | convolution fusion | flops 4836163584 | bytes 40894464 | tf_op jit(solution)/shard_map/dot_general | solution.py:34
  27.1 19.3 %convolution_bitcast_fusion = f32[6144,128]{0,1:T(8,128)} fusion(bf16[128,3072]{1,0:T(8,128)(2,1)S(1)} %fusion.10, bf16[6144,3072]{1,0:T(8,128)(2,1)} %param.14), kind=kOutput, calls=%fused_computation.16 | convolution fusion | flops 4831838208 | bytes 41680896 | tf_op jit(solution)/shard_map/dot_general | solution.py:39
  46.4 0.0 reduce-scatter.4.cloned.1.call-update
  46.5 0.0 reduce-scatter.6.cloned.1.call-start
  46.5 17.7 %convert_bitcast_fusion.1 = bf16[6144,3072]{0,1:T(8,128)(2,1)} fusion(bf16[128,3072]{1,0:T(8,128)(2,1)S(1)} %fusion.10, bf16[128,6144]{1,0:T(8,128)(2,1)} %param.11), kind=kOutput, calls=%fused_computation.1 | convolution fusion | flops 4850712576 | bytes 40108032 | tf_op jit(solution)/shard_map/dot_general | solution.py:24
  64.2 0.0 reduce-scatter.6.cloned.1.call-update
  64.2 0.2 reduce-scatter.8.cloned.1.call-start
  64.5 0.9 copy-done.2
  65.3 15.9 %convert_bitcast_fusion = bf16[6144,3072]{0,1:T(8,128)(2,1)} fusion(bf16[128,6144]{1,0:T(8,128)(2,1)S(1)} %copy-done, bf16[128,3072]{1,0:T(8,128)(2,1)S(1)} %copy-done.2), kind=kOutput, calls=%fused_computation | convolution fusion | flops 4853071872 | bytes 40108032 | tf_op jit(solution)/shard_map/dot_general | solution.py:24
  81.2 0.0 reduce-scatter.8.cloned.1.call-update
  81.2 0.0 copy-start.5
  81.2 9.6 %copy.14 = f32[768,3072]{0,1:T(8,128)} copy(f32[768,3072]{1,0:T(8,128)} %param.16) | data formatting | bytes 18874368 | tf_op args[5]
  90.9 18.9 %reduce-scatter.4.cloned.1.call-done = f32[1536,128]{0,1:T(8,128)} async-done(((f32[6144,128]{0,1:T(8,128)}), f32[1536,128]{0,1:T(8,128)}) %reduce-scatter.4.cloned.1.call-update) | async-done | bytes 786448 | tf_op jit(solution)/shard_map/reduce_scatter | solution.py:38
  109.7 1.9 convert_bitcast_fusion.2
  111.7 227.1 %reduce-scatter.6.cloned.1.call-done = bf16[768,3072]{0,1:T(8,128)(2,1)} async-done(((bf16[6144,3072]{0,1:T(8,128)(2,1)}), bf16[768,3072]{0,1:T(8,128)(2,1)}) %reduce-scatter.6.cloned.1.call-update) | async-done | bytes 4718608 | tf_op jit(solution)/shard_map/reduce_scatter | solution.py:47
  338.7 4.3 fusion.1
  343.0 11.7 %psum.42 = f32[768]{0:T(1024)S(1)} all-reduce(f32[768]{0:T(1024)S(1)} %get-tuple-element.9), channel_id=1, replica_groups=mesh['dp'=8,'mp'=4] {'mp'}, use_global_device_ids=true, to_apply=%region_3.0 | all-reduce | flops 768 | bytes 6144 | tf_op jit(solution)/shard_map/psum | solution.py:62
  354.7 0.0 copy-done.5
  354.7 0.6 fusion.21
  355.3 212.5 %reduce-scatter.8.cloned.1.call-done = bf16[768,3072]{0,1:T(8,128)(2,1)} async-done(((bf16[6144,3072]{0,1:T(8,128)(2,1)}), bf16[768,3072]{0,1:T(8,128)(2,1)}) %reduce-scatter.8.cloned.1.call-update) | async-done | bytes 4718608 | tf_op jit(solution)/shard_map/reduce_scatter | solution.py:51
  567.8 4.3 fusion.6
  572.1 22.9 %all-reduce = (f32[]{:T(128)}, f32[3072]{0:T(1024)S(1)}, f32[3072]{0:T(1024)S(1)}) all-reduce(f32[]{:T(128)} %get-tuple-element.17, f32[3072]{0:T(1024)S(1)} %get-tuple-element.8, f32[3072]{0:T(1024)S(1)} %get-tuple-element.7), channel_id=1, replica_groups=mesh['dp'=8,'mp'=4] {'dp'}, use_global_device_ids=true, to_apply=%region_7.0 | all-reduce | flops 6145 | bytes 49160 | tf_op jit(solution)/shard_map/psum | solution.py:70
  595.0 0.0 copy-done.3
  595.7 10.4 %fusion.4 = f32[768,3072]{0,1:T(8,128)} fusion(f32[768,3072]{0,1:T(8,128)} %copy.14, bf16[768,3072]{0,1:T(8,128)(2,1)} %reduce-scatter.6.cloned.1.call-done, f32[]{:T(128)S(6)} %div.44, f32[3072]{0:T(1024)S(1)} %multiply_add_fusion.1, f32[768]{0:T(1024)S(1)} %get-tuple-element.18), kind=kLoop, calls=%fused_computation.8 | loop fusion | flops 14155776 | bytes 23608324 | tf_op jit(solution)/shard_map/sub | solution.py:74
  606.0 9.6 %copy.15 = f32[768,3072]{1,0:T(8,128)} copy(f32[768,3072]{0,1:T(8,128)} %fusion.4) | data formatting | bytes 18874368
  615.6 0.6 fusion.20
  616.2 12.5 %all-reduce.1 = (f32[]{:T(128)}, f32[768]{0:T(1024)S(1)}) all-reduce(f32[]{:T(128)} %get-tuple-element.15, f32[768]{0:T(1024)S(1)} %get-tuple-element.6), channel_id=1, replica_groups=mesh['dp'=8,'mp'=4] {'mp'}, use_global_device_ids=true, to_apply=%region_14.0 | all-reduce | flops 769 | bytes 6152 | tf_op jit(solution)/shard_map/psum | solution.py:71
  629.4 0.0 copy-start.1
  629.4 10.4 %fusion.9 = f32[3072,768]{1,0:T(8,128)} fusion(f32[3072,768]{1,0:T(8,128)} %param.17, bf16[768,3072]{0,1:T(8,128)(2,1)} %reduce-scatter.8.cloned.1.call-done, f32[]{:T(128)S(6)} %div.50, f32[768]{0:T(1024)S(1)} %multiply_add_fusion.2, f32[3072]{0:T(1024)S(1)} %get-tuple-element.16), kind=kLoop, calls=%fused_computation.15 | loop fusion | flops 14155776 | bytes 23608324 | tf_op jit(solution)/shard_map/sub | solution.py:75
  (9 shorter events, 0.0 us)
Async XLA Ops:
  7.2 1.4 copy-start
  7.2 102.6 %reduce-scatter.4.cloned.1.call-start = ((), (), s32[]{:S(2)}) async-start(), calls=%async_computation.3 | async-start | bytes 3932160 | tf_op jit(solution)/shard_map/reduce_scatter | solution.py:38
  46.5 292.3 %reduce-scatter.6.cloned.1.call-start = ((), (), s32[]{:S(2)}) async-start(), calls=%async_computation.4 | async-start | bytes 42467328 | tf_op jit(solution)/shard_map/reduce_scatter | solution.py:47
  64.2 1.1 copy-start.2
  64.2 503.6 %reduce-scatter.8.cloned.1.call-start = ((), (), s32[]{:S(2)}) async-start(), calls=%async_computation.5 | async-start | bytes 42467328 | tf_op jit(solution)/shard_map/reduce_scatter | solution.py:51
  81.2 273.5 %copy-start.5 = (f32[768]{0:T(1024)S(1)}, f32[768]{0:T(1024)}, u32[]{:S(2)}) copy-start(f32[768]{0:T(1024)} %param.18) | copy-start | bytes 9220
  90.9 504.2 %copy-start.3 = (f32[3072]{0:T(1024)S(1)}, f32[3072]{0:T(1024)}, u32[]{:S(2)}) copy-start(f32[3072]{0:T(1024)} %param.19) | copy-start | bytes 36868
  606.0 9.6 %copy-start.4 = (f32[3072]{0:T(1024)S(1)}, f32[3072]{0:T(1024)}, u32[]{:S(2)}) copy-start(f32[3072]{0:T(1024)} %param.20) | copy-start | bytes 36868
  606.0 22.7 %copy-start.6 = (f32[768]{0:T(1024)S(1)}, f32[768]{0:T(1024)}, u32[]{:S(2)}) copy-start(f32[768]{0:T(1024)} %param.21) | copy-start | bytes 9220
  629.4 10.5 %copy-start.1 = (bf16[128,6144]{1,0:T(8,128)(2,1)S(1)}, bf16[128,6144]{1,0:T(8,128)(2,1)}, u32[]{:S(2)}) copy-start(bf16[128,6144]{1,0:T(8,128)(2,1)} %param.13) | copy-start | bytes 4718596
Sparse Core Ops, SparseCore 0:
  46.6 63.1 reduce-scatter.3
  113.4 225.3 reduce-scatter.5
  342.4 225.4 reduce-scatter.7
where the time goes:
time: 647 us; the launch traced here: 646 us
  waiting for transfers between devices  459 us (71%)
  matrix products  71.4 us (11%)
  blocking collectives  47.1 us (7%)
  other arithmetic  32.4 us (5%)
  local copies, waits for them, and re-layouts  21.5 us (3%)
  between operations  15.1 us (2%)
    reduce_scatter x1, waiting for transfers between devices, body(): lax.psum_scatter(contract_rows(inputs, pre_grad).astype(jnp.bfloat16), 'd...  227 us
    reduce_scatter x1, waiting for transfers between devices, body(): lax.psum_scatter(contract_rows(out_grad, hidden).astype(jnp.bfloat16), 'd...  213 us
    dot_general x2, matrix products, contract_rows(): lax.dot_general(left, right, (((0,), (0,)), ((), ())), preferred_element_...  33.6 us
    psum x1, blocking collectives, body(): mean_in = lax.psum(jnp.sum(rows_in), 'dp') / D  22.9 us
    unnamed x16, local copies, waits for them, and re-layouts  21.5 us
    dot_general x1, matrix products, body(): lax.dot_general(w_in, pre_grad, (((1,), (1,)), ((), ())), preferred_eleme...  19.3 us
    reduce_scatter x1, waiting for transfers between devices, body(): lax.psum_scatter(lax.dot_general(w_in, pre_grad, (((1,), (1,)), ((), ()))...  18.9 us
    dot_general x1, matrix products, body(): lax.dot_general(out_grad, w_out, (((1,), (1,)), ((), ())), preferred_elem...  18.5 us
  transfers between devices with their start and end apart: 3, of which 3 were waited for; matrix products, arithmetic and copies ran while one was open for 8% of the time, Pallas kernels for 0%

commit v1 on v0

v1 whole, which is shorter than its diff:
```python
import math

import jax
import jax.numpy as jnp
from jax import lax
from jax.sharding import PartitionSpec as P

D = 6144
FF = 12288


decay_rate = 0.8
step_size = 0.05
tiny_square = 1e-30


def gelu_parts(pre):
    cumulative = 0.5 * (1.0 + jax.scipy.special.erf(pre * (1.0 / math.sqrt(2.0))))
    density = jnp.exp(-0.5 * pre * pre) * (1.0 / math.sqrt(2.0 * math.pi))
    return (pre * cumulative, cumulative + pre * density)


def contract_rows(left, right):
    return lax.dot_general(
        left, right, (((0,), (0,)), ((), ())), preferred_element_type=jnp.float32
    )


def scatter_sum(partial, axis):
    size = lax.axis_size(axis)
    me = lax.axis_index(axis)
    width = partial.shape[1] // size
    piece = lambda k: lax.dynamic_slice_in_dim(partial, k * width, width, 1)
    total = piece(me)
    for shift in range(1, size):
        moved = piece(lax.rem(me + shift, size)).astype(jnp.bfloat16)
        got = lax.ppermute(moved, axis, [(i, (i + shift) % size) for i in range(size)])
        total = total + got.astype(jnp.float32)
    return total


def body(
    inputs, pre_act, out_grad, w_in, w_out, master_in, master_out, row_in, col_in, row_out, col_out
):
    active, slope = gelu_parts(pre_act.astype(jnp.float32))
    hidden_all = lax.all_gather(active.astype(jnp.bfloat16), "dp", axis=0, tiled=True)
    out_cols = lax.all_to_all(out_grad, "dp", 1, 0, tiled=True)
    in_cols = lax.all_to_all(inputs, "dp", 1, 0, tiled=True)
    hid_grad = lax.dot_general(
        out_grad, w_out, (((1,), (1,)), ((), ())), preferred_element_type=jnp.float32
    )
    pre_grad = (hid_grad * slope).astype(jnp.bfloat16)
    pre_grad_all = lax.all_gather(pre_grad, "dp", axis=0, tiled=True)
    input_part = lax.dot_general(
        pre_grad, w_in, (((1,), (1,)), ((), ())), preferred_element_type=jnp.float32
    )
    input_grad = scatter_sum(input_part, "mp").astype(jnp.bfloat16)
    grad_out = contract_rows(hidden_all, out_cols)
    grad_in = contract_rows(in_cols, pre_grad_all)
    square_in = grad_in * grad_in + tiny_square
    square_out = grad_out * grad_out + tiny_square
    width_in, width_out, row_out_sum = lax.psum(
        (jnp.sum(square_in, axis=1), jnp.sum(square_out, axis=0), jnp.sum(row_out)), "mp"
    )
    rows_in = decay_rate * row_in + (1.0 - decay_rate) * width_in / FF
    cols_out = decay_rate * col_out + (1.0 - decay_rate) * width_out / FF
    hidden_in, hidden_out, sum_in, sum_out = lax.psum(
        (
            jnp.sum(square_in, axis=0),
            jnp.sum(square_out, axis=1),
            jnp.sum(rows_in),
            jnp.sum(width_out),
        ),
        "dp",
    )
    cols_in = decay_rate * col_in + (1.0 - decay_rate) * hidden_in / D
    rows_out = decay_rate * row_out + (1.0 - decay_rate) * hidden_out / D
    mean_in = sum_in / D
    mean_out = (decay_rate * row_out_sum + (1.0 - decay_rate) * sum_out / D) / FF
    update_in = grad_in / jnp.sqrt(rows_in[:, None] * cols_in[None, :] / mean_in)
    update_out = grad_out / jnp.sqrt(rows_out[:, None] * cols_out[None, :] / mean_out)
    new_master_in = master_in - step_size * update_in
    new_master_out = master_out - step_size * update_out
    return (input_grad, new_master_in, new_master_out)


def solution(mesh):
    in_specs = (
        P("dp", None),
        P("dp", "mp"),
        P("dp", None),
        P(None, "mp"),
        P("mp", None),
        P("dp", "mp"),
        P("mp", "dp"),
        P("dp"),
        P("mp"),
        P("mp"),
        P("dp"),
    )
    out_specs = (P("dp", "mp"), P("dp", "mp"), P("mp", "dp"))
    return jax.shard_map(body, mesh=mesh, in_specs=in_specs, out_specs=out_specs, check_vma=False)
```

time: 647 us -> 243 us (0.38)
  waiting for transfers between devices: 459 us -> 60.5 us
  starting transfers between devices: 0.3 us -> 15 us
  blocking collectives: 47.1 us -> 35 us
  matrix products: 71.4 us -> 59.7 us
  local copies, waits for them, and re-layouts: 21.5 us -> 28 us
    reduce_scatter x3 -> x0, waiting for transfers between devices: 458 us -> none  [the longest x1 227 us: body(): lax.psum_scatter(contract_rows(inputs, pre_grad).astype(jnp.bfloat16), 'd...]
    all_to_all x0 -> x2, waiting for transfers between devices: none -> 27.7 us  [the longest x1 27.7 us: body(): in_cols = lax.all_to_all(inputs, 'dp', 1, 0, tiled=True)]
    all_gather x0 -> x2, waiting for transfers between devices: none -> 17.9 us  [the longest x1 17.9 us: body(): lax.all_gather(active.astype(jnp.bfloat16), 'dp', axis=0, tiled=True)]
    ppermute x0 -> x3, waiting for transfers between devices: none -> 14.8 us  [scatter_sum(): lax.ppermute(moved, axis, [(i, (i + shift) % size) for i in range(size)])]
    psum x3 -> x2, blocking collectives: 47.1 us -> 35 us  [the longest x1 22.4 us: body(): lax.psum((jnp.sum(square_in, axis=0), jnp.sum(square_out, axis=1), jnp.su...]
    dot_general x2, matrix products: 33.6 us -> 22.6 us  [contract_rows(): lax.dot_general(left, right, (((0,), (0,)), ((), ())), preferred_element_...]
    all_to_all x0 -> x2, starting transfers between devices: none -> 9.49 us  [the longest x1 5.2 us: body(): in_cols = lax.all_to_all(inputs, 'dp', 1, 0, tiled=True)]
    reduce_sum x4 -> x1, other arithmetic: 9.72 us -> 0.63 us  [body(): jnp.sum(row_out)]
  transfers between devices with their start and end apart: 3 -> 7, of which waited for: 3 -> 3; matrix products, arithmetic and copies ran while one was open for 8% -> 21% of each run, Pallas kernels for 0% -> 0%
where the time goes in v1:
time: 243 us
  waiting for transfers between devices  60.5 us (25%)
  matrix products  59.7 us (25%)
  blocking collectives  35 us (14%)
  other arithmetic  28.4 us (12%)
  local copies, waits for them, and re-layouts  28 us (12%)
  between operations  16.1 us (7%)
  starting transfers between devices  15 us (6%)
    all_to_all x1, waiting for transfers between devices, body(): in_cols = lax.all_to_all(inputs, 'dp', 1, 0, tiled=True)  27.7 us
    unnamed x18, local copies, waits for them, and re-layouts  23.6 us
    dot_general x2, matrix products, contract_rows(): lax.dot_general(left, right, (((0,), (0,)), ((), ())), preferred_element_...  22.6 us
    psum x1, blocking collectives, body(): lax.psum((jnp.sum(square_in, axis=0), jnp.sum(square_out, axis=1), jnp.su...  22.4 us
    dot_general x1, matrix products, body(): lax.dot_general(out_grad, w_out, (((1,), (1,)), ((), ())), preferred_elem...  19.2 us
    dot_general x1, matrix products, body(): lax.dot_general(pre_grad, w_in, (((1,), (1,)), ((), ())), preferred_eleme...  18 us
    all_gather x1, waiting for transfers between devices, body(): lax.all_gather(active.astype(jnp.bfloat16), 'dp', axis=0, tiled=True)  17.9 us
    ppermute x3, waiting for transfers between devices, scatter_sum(): lax.ppermute(moved, axis, [(i, (i + shift) % size) for i in range(size)])  14.8 us
  transfers between devices with their start and end apart: 7, of which 3 were waited for; matrix products, arithmetic and copies ran while one was open for 21% of the time, Pallas kernels for 0%

profile of v1, /device:TPU:0, one launch (start us, length us, event | category | flops | bytes accessed | tf_op | source)
XLA Modules:
  0.0 242.8 jit_solution(6734764929299141886)
XLA Ops:
  7.2 0.0 all-gather.3.cloned.1.call-start
  7.2 19.2 %fusion.7 = bf16[128,3072]{1,0:T(8,128)(2,1)} fusion(bf16[128,6144]{1,0:T(8,128)(2,1)} %param.13, bf16[3072,6144]{1,0:T(8,128)(2,1)} %param.15, bf16[128,3072]{1,0:T(8,128)(2,1)} %param.12), kind=kOutput, calls=%fused_computation.12 | convolution fusion | flops 4836163584 | bytes 40894464 | tf_op jit(solution)/shard_map/dot_general | solution.py:49
  26.5 0.0 all-gather.5.cloned.1.call-start
  26.5 2.5 %fusion.14 = bf16[128,3072]{1,0:T(8,128)(2,1)} fusion(bf16[128,3072]{1,0:T(8,128)(2,1)} %param.12), kind=kLoop, calls=%fused_computation.24 | loop fusion | flops 2359296 | bytes 1572864 | tf_op jit(solution)/shard_map/convert_element_type | solution.py:46
  29.0 0.0 all-gather.5.cloned.1.call-update
  29.0 1.6 copy.18
  30.6 5.2 %all-to-all-start = ((bf16[128,8,768]{0,2,1:T(8,128)(2,1)}), bf16[128,8,768]{0,2,1:T(8,128)(2,1)S(1)}, u32[]{:S(2)}, u32[]{:S(2)}) async-start(bf16[128,8,768]{0,2,1:T(8,128)(2,1)} %bitcast), calls=%async_computation | async-start | bytes 3145728 | tf_op jit(solution)/shard_map/all_to_all | solution.py:48
  35.8 1.7 copy.21
  37.5 27.7 %all-to-all-done = bf16[128,8,768]{0,2,1:T(8,128)(2,1)S(1)} async-done(((bf16[128,8,768]{0,2,1:T(8,128)(2,1)}), bf16[128,8,768]{0,2,1:T(8,128)(2,1)S(1)}, u32[]{:S(2)}, u32[]{:S(2)}) %all-to-all-start) | async-done | bytes 1572896 | tf_op jit(solution)/shard_map/all_to_all | solution.py:48
  65.2 1.1 copy-done
  66.3 4.3 %all-to-all-start.1 = ((bf16[128,8,768]{0,2,1:T(8,128)(2,1)}), bf16[128,8,768]{0,2,1:T(8,128)(2,1)}, u32[]{:S(2)}, u32[]{:S(2)}) async-start(bf16[128,8,768]{0,2,1:T(8,128)(2,1)} %bitcast.4), calls=%async_computation.1 | async-start | bytes 3145728 | tf_op jit(solution)/shard_map/all_to_all | solution.py:47
  70.6 18.0 %fusion.16 = f32[128,6144]{1,0:T(8,128)S(1)} fusion(bf16[128,3072]{1,0:T(8,128)(2,1)} %fusion.7, bf16[6144,3072]{1,0:T(8,128)(2,1)} %param.14), kind=kOutput, calls=%fused_computation.34 | convolution fusion | flops 4831838208 | bytes 41680896 | tf_op jit(solution)/shard_map/dot_general | solution.py:54
  88.6 1.0 dynamic-slice_convert_fusion.2
  89.6 1.6 collective-permute-start
  91.2 2.5 %collective-permute-start.1 = (bf16[128,1536]{1,0:T(8,128)(2,1)}, bf16[128,1536]{1,0:T(8,128)(2,1)}, u32[]{:S(2)}, u32[]{:S(2)}) collective-permute-start(bf16[128,1536]{1,0:T(8,128)(2,1)} %get-tuple-element.27), channel_id=1, source_target_pairs={{0,2},{1,3},{2,0},{3,1},{4,6},{5,7},{6,4},{7,5},{8,10},{9,11},{10,... | collective-permute-start | bytes 1179656 | tf_op jit(solution)/shard_map/ppermute | solution.py:37
  93.7 1.4 collective-permute-start.2
  95.1 9.6 %copy.20 = f32[768,3072]{0,1:T(8,128)} copy(f32[768,3072]{1,0:T(8,128)} %param.16) | data formatting | bytes 18874368 | tf_op args[5]
  104.7 0.6 reduce_sum.68
  105.3 14.8 %collective-permute-done.1 = bf16[128,1536]{1,0:T(8,128)(2,1)} collective-permute-done((bf16[128,1536]{1,0:T(8,128)(2,1)}, bf16[128,1536]{1,0:T(8,128)(2,1)}, u32[]{:S(2)}, u32[]{:S(2)}) %collective-permute-start.1) | collective-permute-done | bytes 393248 | tf_op jit(solution)/shard_map/ppermute | solution.py:37
  120.1 2.2 add_convert_fusion
  122.3 1.7 copy.19
  124.0 1.7 copy.22
  125.7 0.0 all-gather.3.cloned.1.call-done
  125.8 11.3 %fusion.5 = (f32[3072]{0:T(1024)S(1)}, f32[768]{0:T(1024)S(1)}, f32[3072,768]{1,0:T(8,128)}) fusion(bf16[1024,3072]{1,0:T(8,128)(2,1)} %all-gather.3.cloned.1.call-done, bf16[1024,768]{1,0:T(8,128)(2,1)S(1)} %bitcast.29), kind=kOutput, calls=%fused_computation.9 | convolution fusion | flops 4841271296 | bytes 17316864 | tf_op jit(solution)/shard_map/dot_general | solution.py:24
  137.0 17.9 %all-gather.5.cloned.1.call-done = bf16[1024,3072]{1,0:T(8,128)(2,1)} async-done(((bf16[128,3072]{1,0:T(8,128)(2,1)}), bf16[1024,3072]{1,0:T(8,128)(2,1)}) %all-gather.5.cloned.1.call-update) | async-done | bytes 6291472 | tf_op jit(solution)/shard_map/all_gather | solution.py:46
  155.0 11.3 %fusion.4 = (f32[3072]{0:T(1024)S(1)}, f32[768]{0:T(1024)S(1)}, f32[3072,768]{1,0:T(8,128)}) fusion(bf16[1024,3072]{1,0:T(8,128)(2,1)} %all-gather.5.cloned.1.call-done, bf16[1024,768]{1,0:T(8,128)(2,1)S(1)} %bitcast.28), kind=kOutput, calls=%fused_computation.8 | convolution fusion | flops 4841271296 | bytes 17316864 | tf_op jit(solution)/shard_map/dot_general | solution.py:24
  166.2 12.6 %all-reduce.1 = (f32[768]{0:T(1024)S(1)}, f32[768]{0:T(1024)S(1)}, f32[]{:T(128)}) all-reduce(f32[768]{0:T(1024)S(1)} %get-tuple-element.15, f32[768]{0:T(1024)S(1)} %get-tuple-element.13, f32[]{:T(128)} %reduce_sum.68), channel_id=1, replica_groups=mesh['dp'=8,'mp'=4] {'mp'}, use_global_device_ids=true, to_apply=%region_1.0 | all-reduce | flops 1537 | bytes 12296 | tf_op jit(solution)/shard_map/psum | solution.py:62
  178.8 0.7 multiply_add_fusion.3
  179.5 22.4 %all-reduce = (f32[]{:T(128)}, f32[3072]{0:T(1024)S(1)}, f32[]{:T(128)}, f32[3072]{0:T(1024)S(1)}) all-reduce(f32[]{:T(128)} %get-tuple-element.32, f32[3072]{0:T(1024)S(1)} %get-tuple-element.14, f32[]{:T(128)} %get-tuple-element.29, f32[3072]{0:T(1024)S(1)} %get-tuple-element.12), channel_id=1, replica_groups=mesh['dp'=8,'mp'=4] {'dp'}, use_global_device_ids=true, to_apply=%region_5.0 | all-reduce | flops 6146 | bytes 49168 | tf_op jit(solution)/shard_map/psum | solution.py:67
  202.6 11.2 %fusion.2 = f32[768,3072]{0,1:T(8,128)} fusion(f32[768,3072]{0,1:T(8,128)} %copy.20, f32[3072,768]{1,0:T(8,128)} %get-tuple-element.30, f32[]{:T(128)S(6)} %div.47, f32[3072]{0:T(1024)S(1)} %multiply_add_fusion.2, f32[768]{0:T(1024)S(1)} %get-tuple-element.33), kind=kLoop, calls=%fused_computation.4 | loop fusion | flops 11796480 | bytes 28326916 | tf_op jit(solution)/shard_map/sub | solution.py:82
  213.8 9.6 %copy.23 = f32[768,3072]{1,0:T(8,128)} copy(f32[768,3072]{0,1:T(8,128)} %fusion.2) | data formatting | bytes 18874368
  224.7 11.3 %multiply_subtract_fusion = f32[3072,768]{1,0:T(8,128)} fusion(f32[3072,768]{1,0:T(8,128)} %param.17, f32[3072,768]{1,0:T(8,128)} %get-tuple-element.31, f32[]{:T(128)S(6)} %div.54, f32[768]{0:T(1024)S(1)} %get-tuple-element.28, f32[3072]{0:T(1024)S(1)} %multiply_add_fusion.1), kind=kLoop, calls=%fused_computation.5 | loop fusion | flops 11796480 | bytes 28326916 | tf_op jit(solution)/shard_map/sub | solution.py:83
  (19 shorter events, 0.1 us)
Async XLA Ops:
  7.2 21.9 %copy-start.1 = (bf16[128,6144]{1,0:T(8,128)(2,1)S(1)}, bf16[128,6144]{1,0:T(8,128)(2,1)}, u32[]{:S(2)}) copy-start(bf16[128,6144]{1,0:T(8,128)(2,1)} %param.11) | copy-start | bytes 4718596
  7.2 118.6 %all-gather.3.cloned.1.call-start = ((), (), s32[]{:S(2)}) async-start(), calls=%async_computation.2 | async-start | bytes 7077888 | tf_op jit(solution)/shard_map/all_gather | solution.py:53
  26.4 9.4 %copy-start.2 = (bf16[128,6144]{1,0:T(8,128)(2,1)S(1)}, bf16[128,6144]{1,0:T(8,128)(2,1)}, u32[]{:S(2)}) copy-start(bf16[128,6144]{1,0:T(8,128)(2,1)} %param.13) | copy-start | bytes 4718596
  26.5 128.5 %all-gather.5.cloned.1.call-start = ((), (), s32[]{:S(2)}) async-start(), calls=%async_computation.3 | async-start | bytes 7077888 | tf_op jit(solution)/shard_map/all_gather | solution.py:46
  30.6 34.6 %all-to-all-start = ((bf16[128,8,768]{0,2,1:T(8,128)(2,1)}), bf16[128,8,768]{0,2,1:T(8,128)(2,1)S(1)}, u32[]{:S(2)}, u32[]{:S(2)}) async-start(bf16[128,8,768]{0,2,1:T(8,128)(2,1)} %bitcast), calls=%async_computation | async-start | bytes 3145728 | tf_op jit(solution)/shard_map/all_to_all | solution.py:48
  65.2 1.1 copy-start
  66.3 57.7 %all-to-all-start.1 = ((bf16[128,8,768]{0,2,1:T(8,128)(2,1)}), bf16[128,8,768]{0,2,1:T(8,128)(2,1)}, u32[]{:S(2)}, u32[]{:S(2)}) async-start(bf16[128,8,768]{0,2,1:T(8,128)(2,1)} %bitcast.4), calls=%async_computation.1 | async-start | bytes 3145728 | tf_op jit(solution)/shard_map/all_to_all | solution.py:47
  89.6 15.7 %collective-permute-start = (bf16[128,1536]{1,0:T(8,128)(2,1)}, bf16[128,1536]{1,0:T(8,128)(2,1)}, u32[]{:S(2)}, u32[]{:S(2)}) collective-permute-start(bf16[128,1536]{1,0:T(8,128)(2,1)} %get-tuple-element.25), channel_id=1, source_target_pairs={{0,1},{1,2},{2,3},{3,0},{4,5},{5,6},{6,7},{7,4},{8,9},{9,10},{10,1... | collective-permute-start | bytes 1179656 | tf_op jit(solution)/shard_map/ppermute | solution.py:37
  91.2 28.9 %collective-permute-start.1 = (bf16[128,1536]{1,0:T(8,128)(2,1)}, bf16[128,1536]{1,0:T(8,128)(2,1)}, u32[]{:S(2)}, u32[]{:S(2)}) collective-permute-start(bf16[128,1536]{1,0:T(8,128)(2,1)} %get-tuple-element.27), channel_id=1, source_target_pairs={{0,2},{1,3},{2,0},{3,1},{4,6},{5,7},{6,4},{7,5},{8,10},{9,11},{10,... | collective-permute-start | bytes 1179656 | tf_op jit(solution)/shard_map/ppermute | solution.py:37
  93.7 26.4 %collective-permute-start.2 = (bf16[128,1536]{1,0:T(8,128)(2,1)S(1)}, bf16[128,1536]{1,0:T(8,128)(2,1)}, u32[]{:S(2)}, u32[]{:S(2)}) collective-permute-start(bf16[128,1536]{1,0:T(8,128)(2,1)S(1)} %get-tuple-element.26), channel_id=1, source_target_pairs={{0,3},{1,0},{2,1},{3,2},{4,7},{5,4},{6,5},{7,6},{8,11},{9,8},{10,9... | collective-permute-start | bytes 1179656 | tf_op jit(solution)/shard_map/ppermute | solution.py:37
  95.1 9.6 %copy-start.3 = (f32[3072]{0:T(1024)S(1)}, f32[3072]{0:T(1024)}, u32[]{:S(2)}) copy-start(f32[3072]{0:T(1024)} %param.20) | copy-start | bytes 36868
  155.0 23.9 %copy-start.5 = (f32[768]{0:T(1024)S(1)}, f32[768]{0:T(1024)}, u32[]{:S(2)}) copy-start(f32[768]{0:T(1024)} %param.21) | copy-start | bytes 9220
  155.0 23.9 %copy-start.6 = (f32[768]{0:T(1024)S(1)}, f32[768]{0:T(1024)}, u32[]{:S(2)}) copy-start(f32[768]{0:T(1024)} %param.18) | copy-start | bytes 9220
  155.0 47.0 %copy-start.4 = (f32[3072]{0:T(1024)S(1)}, f32[3072]{0:T(1024)}, u32[]{:S(2)}) copy-start(f32[3072]{0:T(1024)} %param.19) | copy-start | bytes 36868
Sparse Core Ops, SparseCore 0:
  26.6 79.3 all-gather.2
  107.8 47.0 all-gather.4

commit v2 on v1

v2 whole, which is shorter than its diff:
```python
import math

import jax
import jax.numpy as jnp
from jax import lax
from jax.experimental.layout import Layout, with_layout_constraint
from jax.sharding import PartitionSpec as P

D = 6144
FF = 12288


decay_rate = 0.8
step_size = 0.05
tiny_square = 1e-30


def gelu_parts(pre):
    cumulative = 0.5 * (1.0 + jax.scipy.special.erf(pre * (1.0 / math.sqrt(2.0))))
    density = jnp.exp(-0.5 * pre * pre) * (1.0 / math.sqrt(2.0 * math.pi))
    return (pre * cumulative, cumulative + pre * density)


def contract_rows(left, right):
    return lax.dot_general(
        left, right, (((0,), (0,)), ((), ())), preferred_element_type=jnp.float32
    )


def scatter_pieces(partial, axis):
    size = lax.axis_size(axis)
    me = lax.axis_index(axis)
    width = partial.shape[1] // size
    piece = lambda k: lax.dynamic_slice_in_dim(partial, k * width, width, 1)
    pieces = [piece(me)]
    for shift in range(1, size):
        moved = piece(lax.rem(me + shift, size)).astype(jnp.bfloat16)
        pieces.append(lax.ppermute(moved, axis, [(i, (i + shift) % size) for i in range(size)]))
    return pieces


def body(
    inputs, pre_act, out_grad, w_in, w_out, master_in, master_out, row_in, col_in, row_out, col_out
):
    active, slope = gelu_parts(pre_act.astype(jnp.float32))
    hidden = active.astype(jnp.bfloat16)
    hidden_all = lax.all_gather(hidden, "dp", axis=0, tiled=True)
    out_grad, _ = lax.optimization_barrier((out_grad, hidden))
    out_cols = lax.all_to_all(out_grad, "dp", 1, 0, tiled=True)
    hid_grad = lax.dot_general(
        out_grad, w_out, (((1,), (1,)), ((), ())), preferred_element_type=jnp.float32
    )
    pre_grad = (hid_grad * slope).astype(jnp.bfloat16)
    pre_grad_all = lax.all_gather(pre_grad, "dp", axis=0, tiled=True)
    input_part = lax.dot_general(
        pre_grad, w_in, (((1,), (1,)), ((), ())), preferred_element_type=jnp.float32
    )
    inputs, input_part = lax.optimization_barrier((inputs, input_part))
    in_cols = lax.all_to_all(inputs, "dp", 1, 0, tiled=True)
    pieces = scatter_pieces(input_part, "mp")

    grad_out = contract_rows(hidden_all, out_cols)
    square_out = grad_out * grad_out + tiny_square
    width_out, row_out_sum = lax.psum((jnp.sum(square_out, axis=0), jnp.sum(row_out)), "mp")
    cols_out = decay_rate * col_out + (1.0 - decay_rate) * width_out / FF
    hidden_out, sum_out = lax.psum((jnp.sum(square_out, axis=1), jnp.sum(width_out)), "dp")
    rows_out = decay_rate * row_out + (1.0 - decay_rate) * hidden_out / D
    mean_out = (decay_rate * row_out_sum + (1.0 - decay_rate) * sum_out / D) / FF
    update_out = grad_out / jnp.sqrt(rows_out[:, None] * cols_out[None, :] / mean_out)
    new_master_out = master_out - step_size * update_out

    pre_grad_all, new_master_out, pieces = lax.optimization_barrier(
        (pre_grad_all, new_master_out, pieces)
    )
    input_grad = sum(piece.astype(jnp.float32) for piece in pieces).astype(jnp.bfloat16)
    grad_in = with_layout_constraint(contract_rows(in_cols, pre_grad_all), Layout((0, 1)))
    square_in = grad_in * grad_in + tiny_square
    width_in = lax.psum(jnp.sum(square_in, axis=1), "mp")
    rows_in = decay_rate * row_in + (1.0 - decay_rate) * width_in / FF
    hidden_in, sum_in = lax.psum((jnp.sum(square_in, axis=0), jnp.sum(rows_in)), "dp")
    cols_in = decay_rate * col_in + (1.0 - decay_rate) * hidden_in / D
    mean_in = sum_in / D
    update_in = grad_in / jnp.sqrt(rows_in[:, None] * cols_in[None, :] / mean_in)
    new_master_in = master_in - step_size * update_in
    return (input_grad, new_master_in, new_master_out)


def solution(mesh):
    in_specs = (
        P("dp", None),
        P("dp", "mp"),
        P("dp", None),
        P(None, "mp"),
        P("mp", None),
        P("dp", "mp"),
        P("mp", "dp"),
        P("dp"),
        P("mp"),
        P("mp"),
        P("dp"),
    )
    out_specs = (P("dp", "mp"), P("dp", "mp"), P("mp", "dp"))
    return jax.shard_map(body, mesh=mesh, in_specs=in_specs, out_specs=out_specs, check_vma=False)
```

time: 243 us -> 234 us (0.963)
  blocking collectives: 35 us -> 67.5 us
  waiting for transfers between devices: 60.5 us -> 34.3 us
  local copies, waits for them, and re-layouts: 28 us -> 10.5 us
    psum x2 -> x4, blocking collectives: 35 us -> 67.5 us  [the longest x1 23.4 us: body(): lax.psum((jnp.sum(square_out, axis=1), jnp.sum(width_out)), 'dp')]
    unnamed x18 -> x12, local copies, waits for them, and re-layouts: 23.6 us -> 0.04 us
    all_gather x1, waiting for transfers between devices: 17.9 us -> 0.02 us  [body(): hidden_all = lax.all_gather(hidden, 'dp', axis=0, tiled=True)]
    ppermute x3, waiting for transfers between devices: 14.8 us -> 0.01 us  [scatter_pieces(): lax.ppermute(moved, axis, [(i, (i + shift) % size) for i in range(size)])]
    all_to_all x1, waiting for transfers between devices: 0.01 us -> 14.5 us  [body(): out_cols = lax.all_to_all(out_grad, 'dp', 1, 0, tiled=True)]
    all_to_all x1, waiting for transfers between devices: 27.7 us -> 19.7 us  [body(): in_cols = lax.all_to_all(inputs, 'dp', 1, 0, tiled=True)]
    optimization_barrier x0 -> x2, local copies, waits for them, and re-layouts: none -> 4.14 us  [the longest x1 2.58 us: body(): inputs, input_part = lax.optimization_barrier((inputs, input_part))]
    dot_general x1, matrix products: 19.2 us -> 22.5 us  [body(): lax.dot_general(out_grad, w_out, (((1,), (1,)), ((), ())), preferred_elem...]
  transfers between devices with their start and end apart: 7 -> 7, of which waited for: 3 -> 2; matrix products, arithmetic and copies ran while one was open for 21% -> 32% of each run, Pallas kernels for 0% -> 0%
where the time goes in v2:
time: 234 us
  blocking collectives  67.5 us (29%)
  matrix products  62.1 us (27%)
  waiting for transfers between devices  34.3 us (15%)
  other arithmetic  29.2 us (12%)
  between operations  16.2 us (7%)
  starting transfers between devices  14 us (6%)
  local copies, waits for them, and re-layouts  10.5 us (4%)
    psum x1, blocking collectives, body(): lax.psum((jnp.sum(square_out, axis=1), jnp.sum(width_out)), 'dp')  23.4 us
    psum x1, blocking collectives, body(): lax.psum((jnp.sum(square_in, axis=0), jnp.sum(rows_in)), 'dp')  23.4 us
    dot_general x1, matrix products, body(): lax.dot_general(out_grad, w_out, (((1,), (1,)), ((), ())), preferred_elem...  22.5 us
    dot_general x2, matrix products, contract_rows(): lax.dot_general(left, right, (((0,), (0,)), ((), ())), preferred_element_...  21.7 us
    all_to_all x1, waiting for transfers between devices, body(): in_cols = lax.all_to_all(inputs, 'dp', 1, 0, tiled=True)  19.7 us
    dot_general x1, matrix products, body(): lax.dot_general(pre_grad, w_in, (((1,), (1,)), ((), ())), preferred_eleme...  17.9 us
    all_to_all x1, waiting for transfers between devices, body(): out_cols = lax.all_to_all(out_grad, 'dp', 1, 0, tiled=True)  14.5 us
    psum x1, blocking collectives, body(): lax.psum((jnp.sum(square_out, axis=0), jnp.sum(row_out)), 'mp')  12.4 us
  transfers between devices with their start and end apart: 7, of which 2 were waited for; matrix products, arithmetic and copies ran while one was open for 32% of the time, Pallas kernels for 0%

profile of v2, /device:TPU:0, one launch (start us, length us, event | category | flops | bytes accessed | tf_op | source)
XLA Modules:
  0.0 233.9 jit_solution(13261236055143968567)
XLA Ops:
  7.2 0.0 all-gather.5.cloned.1.call-start
  7.2 2.4 %fusion.8 = bf16[128,3072]{1,0:T(8,128)(2,1)} fusion(bf16[128,3072]{1,0:T(8,128)(2,1)} %param.12), kind=kLoop, calls=%fused_computation.18 | loop fusion | flops 2359296 | bytes 1572864 | tf_op jit(solution)/shard_map/convert_element_type | solution.py:46
  9.6 0.0 all-gather.5.cloned.1.call-update
  9.6 0.0 all-gather.3.cloned.1.call-start
  9.7 22.5 %fusion.4 = bf16[128,3072]{1,0:T(8,128)(2,1)} fusion(bf16[128,6144]{1,0:T(8,128)(2,1)} %param.13, bf16[3072,6144]{1,0:T(8,128)(2,1)} %param.15, bf16[128,3072]{1,0:T(8,128)(2,1)} %param.12), kind=kOutput, calls=%fused_computation.9 | convolution fusion | flops 4836163584 | bytes 40894464 | tf_op jit(solution)/shard_map/dot_general | solution.py:50
  32.2 1.6 copy.14
  33.8 5.2 %all-to-all-start = ((bf16[128,8,768]{0,2,1:T(8,128)(2,1)}), bf16[128,8,768]{0,2,1:T(8,128)(2,1)}, u32[]{:S(2)}, u32[]{:S(2)}) async-start(bf16[128,8,768]{0,2,1:T(8,128)(2,1)} %bitcast), calls=%async_computation | async-start | bytes 3145728 | tf_op jit(solution)/shard_map/all_to_all | solution.py:49
  39.0 17.9 %fusion.13 = f32[128,6144]{1,0:T(8,128)S(1)} fusion(bf16[128,3072]{1,0:T(8,128)(2,1)} %fusion.4, bf16[6144,3072]{1,0:T(8,128)(2,1)} %param.14), kind=kOutput, calls=%fused_computation.32 | convolution fusion | flops 4831838208 | bytes 41680896 | tf_op jit(solution)/shard_map/dot_general | solution.py:55
  57.0 2.6 %copy.16 = bf16[128,6144]{0,1:T(8,128)(2,1)} copy(bf16[128,6144]{1,0:T(8,128)(2,1)} %param.11) | data formatting | bytes 3145728 | tf_op jit(solution)/shard_map/optimization_barrier | solution.py:58
  59.5 14.5 %all-to-all-done = bf16[128,8,768]{0,2,1:T(8,128)(2,1)} async-done(((bf16[128,8,768]{0,2,1:T(8,128)(2,1)}), bf16[128,8,768]{0,2,1:T(8,128)(2,1)}, u32[]{:S(2)}, u32[]{:S(2)}) %all-to-all-start) | async-done | bytes 1572896 | tf_op jit(solution)/shard_map/all_to_all | solution.py:49
  74.1 4.3 %all-to-all-start.1 = ((bf16[128,8,768]{0,2,1:T(8,128)(2,1)}), bf16[128,8,768]{0,2,1:T(8,128)(2,1)}, u32[]{:S(2)}, u32[]{:S(2)}) async-start(bf16[128,8,768]{0,2,1:T(8,128)(2,1)} %bitcast.14), calls=%async_computation.1 | async-start | bytes 3145728 | tf_op jit(solution)/shard_map/all_to_all | solution.py:59
  78.4 1.1 dynamic-slice_convert_fusion
  79.4 3.3 %collective-permute-start.2 = (bf16[128,1536]{1,0:T(8,128)(2,1)}, bf16[128,1536]{1,0:T(8,128)(2,1)S(1)}, u32[]{:S(2)}, u32[]{:S(2)}) collective-permute-start(bf16[128,1536]{1,0:T(8,128)(2,1)} %get-tuple-element.33), channel_id=1, source_target_pairs={{0,3},{1,0},{2,1},{3,2},{4,7},{5,4},{6,5},{7,6},{8,11},{9,8},{10,9... | collective-permute-start | bytes 1179656 | tf_op jit(solution)/shard_map/ppermute | solution.py:38
  82.8 1.1 collective-permute-start
  83.9 0.6 reduce_sum.65
  84.5 1.0 constant_dynamic-slice_fusion
  85.4 2.6 %copy.15 = bf16[8,128,768]{2,1,0:T(8,128)(2,1)} copy(bf16[8,128,768]{1,2,0:T(8,128)(2,1)} %bitcast.1) | data formatting | bytes 3145728 | tf_op jit(solution)/shard_map/all_to_all | solution.py:49
  88.0 19.7 %all-to-all-done.1 = bf16[128,8,768]{0,2,1:T(8,128)(2,1)} async-done(((bf16[128,8,768]{0,2,1:T(8,128)(2,1)}), bf16[128,8,768]{0,2,1:T(8,128)(2,1)}, u32[]{:S(2)}, u32[]{:S(2)}) %all-to-all-start.1) | async-done | bytes 1572896 | tf_op jit(solution)/shard_map/all_to_all | solution.py:59
  107.7 1.7 copy.17
  109.5 0.0 all-gather.5.cloned.1.call-done
  109.5 10.4 %fusion.1 = (f32[3072]{0:T(1024)S(1)}, f32[768]{0:T(1024)S(1)}, f32[3072,768]{1,0:T(8,128)}) fusion(bf16[1024,3072]{1,0:T(8,128)(2,1)} %all-gather.5.cloned.1.call-done, bf16[1024,768]{1,0:T(8,128)(2,1)} %bitcast.16), kind=kOutput, calls=%fused_computation.5 | convolution fusion | flops 4841271296 | bytes 17316864 | tf_op jit(solution)/shard_map/dot_general | solution.py:25
  119.9 12.4 %all-reduce.2 = (f32[]{:T(128)}, f32[768]{0:T(1024)S(1)}) all-reduce(f32[]{:T(128)} %reduce_sum.65, f32[768]{0:T(1024)S(1)} %get-tuple-element.24), channel_id=1, replica_groups=mesh['dp'=8,'mp'=4] {'mp'}, use_global_device_ids=true, to_apply=%region_5.0 | all-reduce | flops 769 | bytes 6152 | tf_op jit(solution)/shard_map/psum | solution.py:64
  132.4 0.6 multiply_add_fusion.5
  133.0 23.4 %all-reduce.1 = (f32[]{:T(128)}, f32[3072]{0:T(1024)S(1)}) all-reduce(f32[]{:T(128)} %get-tuple-element.37, f32[3072]{0:T(1024)S(1)} %get-tuple-element.23), channel_id=1, replica_groups=mesh['dp'=8,'mp'=4] {'dp'}, use_global_device_ids=true, to_apply=%region_7.0 | all-reduce | flops 3073 | bytes 24584 | tf_op jit(solution)/shard_map/psum | solution.py:66
  157.7 11.2 %multiply_subtract_fusion.1 = f32[3072,768]{1,0:T(8,128)} fusion(f32[3072,768]{1,0:T(8,128)} %param.17, f32[3072,768]{1,0:T(8,128)} %get-tuple-element.38, f32[]{:T(128)S(6)} %div.48, f32[768]{0:T(1024)S(1)} %get-tuple-element.36, f32[3072]{0:T(1024)S(1)} %multiply_add_fusion.3), kind=kLoop, calls=%fused_computation.2 | loop fusion | flops 11796480 | bytes 28326916 | tf_op jit(solution)/shard_map/sub | solution.py:70
  169.0 0.0 all-gather.3.cloned.1.call-done
  169.0 11.3 %fusion.2 = (f32[3072]{0:T(1024)S(1)}, f32[768]{0:T(1024)S(1)}, f32[768,3072]{1,0:T(8,128)}) fusion(bf16[1024,768]{1,0:T(8,128)(2,1)S(1)} %bitcast.15, bf16[1024,3072]{1,0:T(8,128)(2,1)} %all-gather.3.cloned.1.call-done), kind=kOutput, calls=%fused_computation.6 | convolution fusion | flops 4841271296 | bytes 17316864 | tf_op jit(solution)/shard_map/dot_general | solution.py:25
  180.3 8.3 %psum.53 = f32[768]{0:T(1024)S(1)} all-reduce(f32[768]{0:T(1024)S(1)} %get-tuple-element.22), channel_id=1, replica_groups=mesh['dp'=8,'mp'=4] {'mp'}, use_global_device_ids=true, to_apply=%region_9.0 | all-reduce | flops 768 | bytes 6144 | tf_op jit(solution)/shard_map/psum | solution.py:78
  188.6 0.6 fusion.12
  189.2 23.4 %all-reduce = (f32[]{:T(128)}, f32[3072]{0:T(1024)S(1)}) all-reduce(f32[]{:T(128)} %get-tuple-element.31, f32[3072]{0:T(1024)S(1)} %get-tuple-element.21), channel_id=1, replica_groups=mesh['dp'=8,'mp'=4] {'dp'}, use_global_device_ids=true, to_apply=%region_13.0 | all-reduce | flops 3073 | bytes 24584 | tf_op jit(solution)/shard_map/psum | solution.py:80
  213.3 2.0 add_convert_fusion
  215.3 11.7 %multiply_subtract_fusion = f32[768,3072]{1,0:T(8,128)} fusion(f32[768,3072]{1,0:T(8,128)} %param.16, f32[768,3072]{1,0:T(8,128)} %get-tuple-element.39, f32[]{:T(128)S(6)} %div.54, f32[3072]{0:T(1024)S(1)} %multiply_add_fusion.2, f32[768]{0:T(1024)S(1)} %get-tuple-element.32), kind=kLoop, calls=%fused_computation | loop fusion | flops 11796480 | bytes 28326916 | tf_op jit(solution)/shard_map/sub | solution.py:84
  (19 shorter events, 0.1 us)
Async XLA Ops:
  7.2 102.3 %all-gather.5.cloned.1.call-start = ((), (), s32[]{:S(2)}) async-start(), calls=%async_computation.3 | async-start | bytes 7077888 | tf_op jit(solution)/shard_map/all_gather | solution.py:47
  9.6 22.6 %copy-start.1 = (bf16[128,6144]{1,0:T(8,128)(2,1)S(1)}, bf16[128,6144]{1,0:T(8,128)(2,1)}, u32[]{:S(2)}) copy-start(bf16[128,6144]{1,0:T(8,128)(2,1)} %param.13) | copy-start | bytes 4718596
  9.6 159.4 %all-gather.3.cloned.1.call-start = ((), (), s32[]{:S(2)}) async-start(), calls=%async_computation.2 | async-start | bytes 7077888 | tf_op jit(solution)/shard_map/all_gather | solution.py:54
  33.8 40.2 %all-to-all-start = ((bf16[128,8,768]{0,2,1:T(8,128)(2,1)}), bf16[128,8,768]{0,2,1:T(8,128)(2,1)}, u32[]{:S(2)}, u32[]{:S(2)}) async-start(bf16[128,8,768]{0,2,1:T(8,128)(2,1)} %bitcast), calls=%async_computation | async-start | bytes 3145728 | tf_op jit(solution)/shard_map/all_to_all | solution.py:49
  56.9 26.9 %copy-start.2 = (f32[3072]{0:T(1024)S(1)}, f32[3072]{0:T(1024)}, u32[]{:S(2)}) copy-start(f32[3072]{0:T(1024)} %param.20) | copy-start | bytes 36868
  74.1 33.7 %all-to-all-start.1 = ((bf16[128,8,768]{0,2,1:T(8,128)(2,1)}), bf16[128,8,768]{0,2,1:T(8,128)(2,1)}, u32[]{:S(2)}, u32[]{:S(2)}) async-start(bf16[128,8,768]{0,2,1:T(8,128)(2,1)} %bitcast.14), calls=%async_computation.1 | async-start | bytes 3145728 | tf_op jit(solution)/shard_map/all_to_all | solution.py:59
  79.4 89.5 %collective-permute-start.2 = (bf16[128,1536]{1,0:T(8,128)(2,1)}, bf16[128,1536]{1,0:T(8,128)(2,1)S(1)}, u32[]{:S(2)}, u32[]{:S(2)}) collective-permute-start(bf16[128,1536]{1,0:T(8,128)(2,1)} %get-tuple-element.33), channel_id=1, source_target_pairs={{0,3},{1,0},{2,1},{3,2},{4,7},{5,4},{6,5},{7,6},{8,11},{9,8},{10,9... | collective-permute-start | bytes 1179656 | tf_op jit(solution)/shard_map/ppermute | solution.py:38
  82.8 86.2 %collective-permute-start.1 = (bf16[128,1536]{1,0:T(8,128)(2,1)}, bf16[128,1536]{1,0:T(8,128)(2,1)}, u32[]{:S(2)}, u32[]{:S(2)}) collective-permute-start(bf16[128,1536]{1,0:T(8,128)(2,1)} %get-tuple-element.34), channel_id=1, source_target_pairs={{0,2},{1,3},{2,0},{3,1},{4,6},{5,7},{6,4},{7,5},{8,10},{9,11},{10,... | collective-permute-start | bytes 1179656 | tf_op jit(solution)/shard_map/ppermute | solution.py:38
  82.8 86.2 %collective-permute-start = (bf16[128,1536]{1,0:T(8,128)(2,1)}, bf16[128,1536]{1,0:T(8,128)(2,1)}, u32[]{:S(2)}, u32[]{:S(2)}) collective-permute-start(bf16[128,1536]{1,0:T(8,128)(2,1)} %get-tuple-element.35), channel_id=1, source_target_pairs={{0,1},{1,2},{2,3},{3,0},{4,5},{5,6},{6,7},{7,4},{8,9},{9,10},{10,1... | collective-permute-start | bytes 1179656 | tf_op jit(solution)/shard_map/ppermute | solution.py:38
  109.5 22.9 %copy-start.4 = (f32[768]{0:T(1024)S(1)}, f32[768]{0:T(1024)}, u32[]{:S(2)}) copy-start(f32[768]{0:T(1024)} %param.21) | copy-start | bytes 9220
  169.0 19.6 %copy-start.5 = (f32[768]{0:T(1024)S(1)}, f32[768]{0:T(1024)}, u32[]{:S(2)}) copy-start(f32[768]{0:T(1024)} %param.18) | copy-start | bytes 9220
  169.0 44.2 %copy-start.3 = (f32[3072]{0:T(1024)S(1)}, f32[3072]{0:T(1024)}, u32[]{:S(2)}) copy-start(f32[3072]{0:T(1024)} %param.19) | copy-start | bytes 36868
  169.0 44.2 %copy-start = (f32[128,1536]{1,0:T(8,128)S(1)}, f32[128,1536]{1,0:T(8,128)}, u32[]{:S(2)}) copy-start(f32[128,1536]{1,0:T(8,128)} %constant_dynamic-slice_fusion) | copy-start | bytes 2359300
Sparse Core Ops, SparseCore 0:
  9.9 61.8 all-gather.4
  73.7 59.2 all-gather.2
